TPU v7x, 32 devices: a 4x4x1 block of a 4x4x8 slice. The times are simulated.
32 devices in a mesh: dp: 1 (over z), tp: 32 (over x, y, core).
Axes of the slice: x: 4, y: 4, z: 1, core: 2. Of those that a mesh axis runs over, the one named last changes fastest.
The devices are a block of a 4x4x8 slice.
Arguments:
- x: bfloat16 [4096, 8192], P(('dp', 'tp'))
- dy: bfloat16 [4096, 8192], P(('dp', 'tp'))
- gate: bfloat16 [4096, 24576], P('dp', 'tp')
- up: bfloat16 [4096, 24576], P('dp', 'tp')
- w_gate: bfloat16 [8192, 24576], P(None, 'tp')
- w_up: bfloat16 [8192, 24576], P(None, 'tp')
- w_down: bfloat16 [24576, 8192], P('tp')
Outputs:
- output 1: bfloat16 [4096, 8192], P(('dp', 'tp'))
- output 2: bfloat16 [8192, 24576], P('dp', 'tp')
- output 3: bfloat16 [8192, 24576], P('dp', 'tp')
- output 4: bfloat16 [24576, 8192], P(('dp', 'tp'))
All inputs are finite; a program needn't handle non-finite values.
Results may differ from a plain program's by a relative error of at most 0.012.
Values are sent between devices in bfloat16 or wider.
A program may use at most 768 MiB of HBM per device.

v0:
```python
import jax
import jax.numpy as jnp


def act(gate, up):
    return jax.nn.silu(gate) * up


def solution(mesh):
    def step(x, dy, gate, up, w_gate, w_up, w_down):
        hidden, back = jax.vjp(act, gate.astype(jnp.float32), up.astype(jnp.float32))
        d_hidden = jnp.dot(dy, w_down.T, preferred_element_type=jnp.float32)
        d_gate, d_up = (g.astype(jnp.bfloat16) for g in back(d_hidden))
        dx = jnp.dot(d_gate, w_gate.T) + jnp.dot(d_up, w_up.T)
        groups = mesh.shape["dp"]

        def by_group(a, b):
            a, b = (t.reshape(groups, -1, t.shape[-1]) for t in (a, b))
            product = jnp.einsum("gta,gtb->gab", a, b, preferred_element_type=jnp.float32)
            return product.astype(jnp.bfloat16).reshape(-1, b.shape[-1])

        return dx, by_group(x, d_gate), by_group(x, d_up), by_group(hidden.astype(jnp.bfloat16), dy)

    return step
```

profile of v0, /device:TPU:97, one launch (start us, length us, event | category | flops | bytes accessed | tf_op | source)
XLA Modules:
  0.0 731.2 jit_solution(7622076617171557088)
XLA Ops:
  7.2 0.1 all-gather.7.cloned.1.call-start
  7.2 0.7 all-gather.7.cloned.1.call-update
  8.0 0.1 all-gather.9.cloned.1.call-start
  8.0 0.7 all-gather.9.cloned.1.call-update
  8.8 0.1 reduce-scatter.5.cloned.1.call-start
  8.9 201.4 %all-gather.7.cloned.1.call-done = bf16[4096,8192]{1,0:T(8,128)(2,1)} async-done(((bf16[128,8192]{1,0:T(8,128)(2,1)}), bf16[4096,8192]{1,0:T(8,128)(2,1)}) %all-gather.7.cloned.1.call-update) | async-done | bytes 67108880 | tf_op args[1]
  210.2 65.6 %fusion.6 = (bf16[4096,768]{1,0:T(8,128)(2,1)}, f32[4096,768]{1,0:T(8,128)}) fusion(bf16[4096,768]{1,0:T(8,128)(2,1)} %param.3, bf16[4096,768]{1,0:T(8,128)(2,1)} %param.2, bf16[4096,8192]{1,0:T(8,128)(2,1)} %all-gather.7.cloned.1.call-done, bf16[768,8192]{1,0:T(8,128)(2,1)} %param.1), kind=kOutput, calls=%fused_computation.16 | convolution fusion | flops 51580502016 | bytes 111149056 | tf_op jit(solution)/dot_general | solution.py:12
  275.8 60.6 %fusion.11 = bf16[4096,8192]{1,0:T(8,128)(2,1)} fusion(bf16[4096,768]{1,0:T(8,128)(2,1)} %get-tuple-element.4, bf16[8192,768]{1,0:T(8,128)(2,1)} %param.4), kind=kOutput, calls=%fused_computation.21 | convolution fusion | flops 51539607552 | bytes 85983232 | tf_op jit(solution)/dot_general | solution.py:14
  336.4 104.9 %convolution_add_fusion = bf16[4096,8192]{1,0:T(8,128)(2,1)} fusion(bf16[4096,8192]{1,0:T(8,128)(2,1)} %fusion.11, bf16[8192,768]{1,0:T(8,128)(2,1)} %param.5, f32[4096,768]{1,0:T(8,128)} %get-tuple-element.5, bf16[4096,768]{1,0:T(8,128)(2,1)} %param.3), kind=kOutput, calls=%fused_computation | convolution fusion | flops 51595182080 | bytes 165675008 | tf_op jit(solution)/dot_general | solution.py:14
  441.3 0.1 reduce-scatter.5.cloned.1.call-update
  441.4 0.0 all-gather.9.cloned.1.call-done
  441.4 70.0 %fusion.8 = bf16[8192,768]{0,1:T(8,128)(2,1)} fusion(bf16[4096,8192]{1,0:T(8,128)(2,1)} %all-gather.9.cloned.1.call-done, f32[4096,768]{1,0:T(8,128)} %get-tuple-element.5, bf16[4096,768]{1,0:T(8,128)(2,1)} %param.3), kind=kOutput, calls=%fused_computation.19 | convolution fusion | flops 51567919104 | bytes 98566144 | tf_op jit(solution)/gta,gtb->gab/dot_general | solution.py:19
  511.4 16.6 %copy.1 = bf16[8192,768]{1,0:T(8,128)(2,1)} copy(bf16[8192,768]{0,1:T(8,128)(2,1)} %fusion.8) | data formatting | bytes 25165824
  528.0 60.5 %fusion.7 = bf16[8192,768]{0,1:T(8,128)(2,1)} fusion(bf16[4096,768]{1,0:T(8,128)(2,1)} %get-tuple-element.4, bf16[4096,8192]{1,0:T(8,128)(2,1)} %all-gather.9.cloned.1.call-done), kind=kOutput, calls=%fused_computation.18 | convolution fusion | flops 51545899008 | bytes 85983232 | tf_op jit(solution)/gta,gtb->gab/dot_general | solution.py:19
  588.5 16.6 %copy = bf16[8192,768]{1,0:T(8,128)(2,1)} copy(bf16[8192,768]{0,1:T(8,128)(2,1)} %fusion.7) | data formatting | bytes 25165824
  605.1 69.5 %convolution_convert_fusion = bf16[768,8192]{1,0:T(8,128)(2,1)} fusion(bf16[4096,8192]{1,0:T(8,128)(2,1)} %all-gather.7.cloned.1.call-done, bf16[4096,768]{1,0:T(8,128)(2,1)} %param.2, bf16[4096,768]{1,0:T(8,128)(2,1)} %param.3), kind=kOutput, calls=%fused_computation.7 | convolution fusion | flops 51571064832 | bytes 92274688 | tf_op jit(solution)/gta,gtb->gab/dot_general | solution.py:19
  674.6 49.9 %reduce-scatter.5.cloned.1.call-done = bf16[128,8192]{1,0:T(8,128)(2,1)} async-done(((bf16[4096,8192]{1,0:T(8,128)(2,1)}), bf16[128,8192]{1,0:T(8,128)(2,1)}) %reduce-scatter.5.cloned.1.call-update) | async-done | bytes 2097168
Async XLA Ops:
  7.2 203.1 %all-gather.7.cloned.1.call-start = ((), (), s32[]{:S(2)}) async-start(), calls=%async_computation.1 | async-start | bytes 69206016 | tf_op args[1]
  8.0 433.4 %all-gather.9.cloned.1.call-start = ((), (), s32[]{:S(2)}) async-start(), calls=%async_computation.2 | async-start | bytes 69206016 | tf_op args[0]
  8.8 715.7 %reduce-scatter.5.cloned.1.call-start = ((), (), s32[]{:S(2)}) async-start(), calls=%async_computation.3 | async-start | bytes 69206016
Sparse Core Ops, SparseCore 0:
  10.1 200.1 all-gather.6
  212.3 194.8 all-gather.8
  441.5 282.8 reduce-scatter.4
where the time goes:
time: 741 us; the launch traced here: 731 us
  matrix products  431 us (58%)
  waiting for transfers between devices  253 us (34%)
  local copies, waits for them, and re-layouts  33.2 us (4%)
  between operations  14 us (2%)
    unnamed x6, waiting for transfers between devices  253 us
    dot_general x3, matrix products, by_group(): jnp.einsum('gta,gtb->gab', a, b, preferred_element_type=jnp.float32)  200 us
    dot_general x2, matrix products, step(): dx = jnp.dot(d_gate, w_gate.T) + jnp.dot(d_up, w_up.T)  165 us
    dot_general x1, matrix products, step(): d_hidden = jnp.dot(dy, w_down.T, preferred_element_type=jnp.float32)  65.6 us
    unnamed x2, local copies, waits for them, and re-layouts  33.2 us
  transfers between devices with their start and end apart: 3, of which 2 were waited for; matrix products, arithmetic and copies ran while one was open for 63% of the time, Pallas kernels for 0%

commit v1 on v0

v1 whole, which is shorter than its diff:
```python
import functools
import math

import jax
import jax.numpy as jnp
from jax import lax
from jax.experimental import pallas as pl
from jax.experimental.pallas import tpu as pltpu
from jax.sharding import PartitionSpec as P

F32, BF16 = jnp.float32, jnp.bfloat16
RINGS = 4
HALVES = 2


def act(gate, up):
    return jax.nn.silu(gate) * up


def place(k):
    me = lax.axis_index("tp")
    core, chip = me % 2, me // 2
    a, b = chip // k, chip % k
    s = (a + b) % k
    return core, a, b, (a * k + s, b * k + s)


def chip_at(k, cycle, position):
    a = position // k
    b = (position % k - a + k) % k
    return a * k + b if cycle == 0 else b * k + a


def on_ring(ring, position, steps, chips):
    return (position + steps + chips) % chips if ring % 2 == 0 else (position - steps + chips) % chips


def greet(k, core, a, b):
    chips = (((a + 1) % k) * k + b, ((a + k - 1) % k) * k + b, a * k + (b + 1) % k, a * k + (b + k - 1) % k)
    barrier = pltpu.get_barrier_semaphore()
    for chip in chips:
        pl.semaphore_signal(barrier, inc=1, device_id={"tp": chip * 2 + core})
    pl.semaphore_signal(barrier, inc=1, device_id={"tp": (a * k + b) * 2 + 1 - core})
    pl.semaphore_wait(barrier, 5)


def scatter_kernel(k, dg, du, wg, wu, out, wv, av, own, psend, precv, rsend, rrecv,
                   w_sem, a_sem, psend_sem, precv_sem, rsend_sem, rrecv_sem, out_sem):
    chips = k * k
    units, width, depth = wv.shape
    rows, ff = out.shape[0], depth // 2
    core, a, b, positions = place(k)
    partner = (a * k + b) * 2 + 1 - core
    order = [(r * HALVES + h, r, h) for h in range(HALVES) for r in range(RINGS)]

    def w_copies(u):
        cols = pl.ds(u * width, width)
        return [pltpu.make_async_copy(w.at[cols], wv.at[u, :, pl.ds(i * ff, ff)], w_sem.at[u, i]) for i, w in enumerate((wg, wu))]

    def a_copies(s, r):
        to = chip_at(k, r // 2, on_ring(r, positions[r // 2], -1 - s + chips, chips))
        copies = []
        for i, which in enumerate((core, 1 - core)):
            at = pl.ds((to * 2 + which) * rows, rows)
            for j, d in enumerate((dg, du)):
                copies.append(pltpu.make_async_copy(
                    d.at[at], av.at[s % 2, r, pl.ds(i * rows, rows), pl.ds(j * ff, ff)], a_sem.at[s % 2, r, 2 * i + j]))
        return copies

    def to_partner(s, u):
        return pltpu.make_async_remote_copy(
            psend.at[u], precv.at[s % 2, u], psend_sem.at[u], precv_sem.at[s % 2, u], device_id={"tp": partner})

    def to_next(s, u, r):
        to = chip_at(k, r // 2, on_ring(r, positions[r // 2], 1, chips)) * 2 + core
        return pltpu.make_async_remote_copy(
            rsend.at[s % 2, u], rrecv.at[(s + 1) % 3, u], rsend_sem.at[s % 2, u], rrecv_sem.at[(s + 1) % 3, u], device_id={"tp": to})

    def to_out(u):
        return pltpu.make_async_copy(rsend.at[(chips - 1) % 2, u], out.at[:, pl.ds(u * width, width)], out_sem.at[u])

    def multiply(s, u, r, h, first=False):
        if first:
            for c in w_copies(u):
                c.wait()
        if h == 0:
            for c in a_copies(s, r):
                c.wait()
        if not first:
            to_partner(s, u).wait_send()
        acc = lax.dot_general(av[s % 2, r], wv[u], (((1,), (1,)), ((), ())), preferred_element_type=F32)
        own[u] = acc[:rows]
        psend[u] = acc[rows:].astype(BF16)
        to_partner(s, u).start()

    def combine(s, u, r):
        to_partner(s, u).wait_recv()

        @pl.when(s >= 2)
        def _():
            to_next(s, u, r).wait_send()

        @pl.when(s == 0)
        def _():
            rsend[s % 2, u] = (own[u] + precv[s % 2, u].astype(F32)).astype(BF16)

        @pl.when(s > 0)
        def _():
            to_next(s - 1, u, r).wait_recv()
            rsend[s % 2, u] = (own[u] + precv[s % 2, u].astype(F32) + rrecv[s % 3, u].astype(F32)).astype(BF16)

        @pl.when(s < chips - 1)
        def _():
            to_next(s, u, r).start()

        @pl.when(s == chips - 1)
        def _():
            to_out(u).start()

    for u, r, h in order:
        if h == 0:
            for c in a_copies(0, r):
                c.start()
        for c in w_copies(u):
            c.start()
    for r in range(RINGS):
        for c in a_copies(1, r):
            c.start()
    greet(k, core, a, b)
    for u, r, h in order:
        multiply(0, u, r, h, first=True)

    @pl.loop(0, chips)
    def _(s):
        @pl.when(s + 2 < chips)
        def _():
            for r in range(RINGS):
                for c in a_copies(s + 2, r):
                    c.start()
        for u, r, h in order:
            combine(s, u, r)

            @pl.when(s + 1 < chips)
            def _():
                multiply(s + 1, u, r, h)

    for u, r, h in order:
        to_partner(chips - 1, u).wait_send()
        to_next(chips - 2, u, r).wait_send()
        to_out(u).wait()


def scatter_dx(k, dg, du, wg, wu):
    tokens, ff = dg.shape
    d = wg.shape[0]
    rows = tokens // (2 * k * k)
    units = RINGS * HALVES
    width = d // units
    dma = pltpu.SemaphoreType.DMA
    return pl.pallas_call(
        functools.partial(scatter_kernel, k),
        out_shape=jax.ShapeDtypeStruct((rows, d), BF16),
        in_specs=[pl.BlockSpec(memory_space=pl.ANY)] * 4,
        out_specs=pl.BlockSpec(memory_space=pl.ANY),
        scratch_shapes=[
            pltpu.VMEM((units, width, 2 * ff), BF16),
            pltpu.VMEM((2, RINGS, 2 * rows, 2 * ff), BF16),
            pltpu.VMEM((units, rows, width), F32),
            pltpu.VMEM((units, rows, width), BF16),
            pltpu.VMEM((2, units, rows, width), BF16),
            pltpu.VMEM((2, units, rows, width), BF16),
            pltpu.VMEM((3, units, rows, width), BF16),
            dma((units, 2)), dma((2, RINGS, 4)), dma((units,)), dma((2, units)), dma((2, units)), dma((3, units)), dma((units,)),
        ],
        compiler_params=pltpu.CompilerParams(collective_id=0, has_side_effects=True, vmem_limit_bytes=63 * 2**20),
        cost_estimate=pl.CostEstimate(flops=4 * tokens * ff * d, bytes_accessed=6 * tokens * ff + 4 * d * ff, transcendentals=0),
        name="scatter_dx",
    )(dg, du, wg, wu)


SLOTS = 4


def gather(k, passes, core, a, b, positions, src, slots, load_sem, next_sem, ring_sem, mate_send_sem, mate_sem, credit, before, pieces, after):
    chips = k * k
    total = passes * chips
    share, cols = slots.shape[1] // (2 * RINGS), slots.shape[2]
    width = cols // HALVES
    partner = (a * k + b) * 2 + 1 - core

    def part(g, r, h, which=core):
        at = pl.multiple_of((2 * r + which) * share, share)
        return slots.at[g % SLOTS, pl.ds(at, share), pl.ds(h * width, width)]

    def load(g, r, h):
        at = pl.multiple_of(g // chips * cols + h * width, width)
        return pltpu.make_async_copy(src.at[pl.ds(r * share, share), pl.ds(at, width)], part(g, r, h), load_sem.at[r, h])

    def to_next(g, r, h):
        to = chip_at(k, r // 2, on_ring(r, positions[r // 2], 1, chips)) * 2 + core
        return pltpu.make_async_remote_copy(
            part(g, r, h), part(g + 1, r, h), next_sem.at[g % 2, r, h], ring_sem.at[(g + 1) % SLOTS, r, h], device_id={"tp": to})

    def to_mate(g, r, h):
        return pltpu.make_async_remote_copy(
            part(g, r, h), part(g, r, h), mate_send_sem.at[g % 2, r, h], mate_sem.at[g % SLOTS, r, h], device_id={"tp": partner})

    def came_from_mate(g, r, h):
        return pltpu.make_async_remote_copy(
            part(g, r, h), part(g, r, h, 1 - core), mate_send_sem.at[g % 2, r, h], mate_sem.at[g % SLOTS, r, h], device_id={"tp": partner})

    def pass_on(g, r, h):
        @pl.when(g % chips == 0)
        def _():
            load(g, r, h).wait()

        @pl.when(g % chips > 0)
        def _():
            to_next(g - 1, r, h).wait_recv()

        @pl.when(g % chips < chips - 1)
        def _():
            if h == 0:
                @pl.when(g + 1 >= SLOTS)
                def _():
                    pl.semaphore_wait(credit.at[r], 1)
            to_next(g, r, h).start()
        to_mate(g, r, h).start()

    both = [(r, h) for h in range(HALVES) for r in range(RINGS)]
    for r, h in both:
        load(0, r, h).start()
    greet(k, core, a, b)

    @pl.loop(0, total + 1)
    def _(g):
        for h in range(HALVES):
            @pl.when(g < total)
            def _():
                for r in range(RINGS):
                    pass_on(g, r, h)

            @pl.when(g > 0)
            def _():
                if h == 0:
                    for r, half in both:
                        came_from_mate(g - 1, r, half).wait_recv()
                    before(g - 1)
                pieces[h](g - 1)

        @pl.when(g > 0)
        def _():
            after(g - 1)
            for r, h in both:
                @pl.when((g - 1) % chips < chips - 1)
                def _():
                    to_next(g - 1, r, h).wait_send()
                to_mate(g - 1, r, h).wait_send()
            refill = g - 1 + SLOTS

            @pl.when(jnp.logical_and(refill < total, refill % chips > 0))
            def _():
                for r in range(RINGS):
                    frm = chip_at(k, r // 2, on_ring(r, positions[r // 2], -1, chips)) * 2 + core
                    pl.semaphore_signal(credit.at[r], inc=1, device_id={"tp": frm})

            @pl.when(jnp.logical_and(refill < total, refill % chips == 0))
            def _():
                for r, h in both:
                    load(refill, r, h).start()


def gather_scratch(rows, cols):
    dma, two = pltpu.SemaphoreType.DMA, (2, RINGS, HALVES)
    return [
        pltpu.VMEM((SLOTS, 2 * rows, cols), BF16),
        dma((RINGS, HALVES)), dma(two), dma((SLOTS, RINGS, HALVES)), dma(two), dma((SLOTS, RINGS, HALVES)),
        pltpu.SemaphoreType.REGULAR((RINGS,)),
    ]


def token_rows(k, positions, g, share, rows):
    chips = k * k
    for r in range(RINGS):
        chip = chip_at(k, r // 2, on_ring(r, positions[r // 2], -(g % chips), chips))
        for c in range(2):
            yield (2 * r + c) * share, pl.multiple_of((chip * 2 + c) * rows + r * share, share)


def hidden_kernel(k, dy, gate, up, w_down, dg, du, dw, wd, wacc, hacc, given, hid, grads, *rest):
    (w_sem, given_sem, grads_sem, out_sem), comm = rest[:4], rest[4:]
    slots = comm[0]
    chips, (rows, d), ff = k * k, dy.shape, gate.shape[1]
    share = rows // RINGS
    core, a, b, positions = place(k)
    quarter = d // 4
    block = quarter // 4

    def given_copies(g):
        return [
            pltpu.make_async_copy(t.at[pl.ds(at, share)], given.at[g % 2, j, pl.ds(to, share)], given_sem.at[g % 2, j, i])
            for i, (to, at) in enumerate(token_rows(k, positions, g, share, rows)) for j, t in enumerate((gate, up))]

    def grads_copies(g):
        return [
            pltpu.make_async_copy(grads.at[g % 2, j, pl.ds(to, share)], t.at[pl.ds(at, share)], grads_sem.at[g % 2, j, i])
            for i, (to, at) in enumerate(token_rows(k, positions, g, share, rows)) for j, t in enumerate((dg, du))]

    w_copies = [pltpu.make_async_copy(w_down.at[:, pl.ds(i * quarter, quarter)], wd.at[i], w_sem.at[i]) for i in range(4)]
    for c in w_copies:
        c.start()
    for c in given_copies(0):
        c.start()

    @pl.loop(0, ff, step=64)
    def _(i):
        wacc[pl.ds(pl.multiple_of(i, 64), 64)] = jnp.zeros((64, d), F32)

    def before(g):
        @pl.when(g == 0)
        def _():
            for c in w_copies:
                c.wait()

        @pl.when(g + 1 < chips)
        def _():
            for c in given_copies(g + 1):
                c.start()

    def d_hidden(g):
        for i in range(4):
            term = lax.dot_general(slots[g % SLOTS, :, pl.ds(i * quarter, quarter)], wd[i], (((1,), (1,)), ((), ())), preferred_element_type=F32)
            hacc[...] = term if i == 0 else hacc[...] + term
        for c in given_copies(g):
            c.wait()

        @pl.when(g >= 2)
        def _():
            for c in grads_copies(g - 2):
                c.wait()

        @pl.loop(0, 2 * rows, step=2 * share)
        def _(i):
            at = pl.ds(pl.multiple_of(i, 2 * share), 2 * share)
            hidden, back = jax.vjp(act, given[g % 2, 0, at].astype(F32), given[g % 2, 1, at].astype(F32))
            for j, t in enumerate(back(hacc[at])):
                grads[g % 2, j, at] = t.astype(BF16)
            hid[at] = hidden.astype(BF16)
        for c in grads_copies(g):
            c.start()

    def d_down(g):
        @pl.loop(0, d, step=block)
        def _(i):
            at = pl.ds(pl.multiple_of(i, block), block)
            wacc[:, at] += lax.dot_general(hid[...], slots[g % SLOTS, :, at], (((0,), (0,)), ((), ())), preferred_element_type=F32)

    gather(k, 1, core, a, b, positions, dy, *comm, before, (d_hidden, d_down), lambda g: None)
    out_copies = []
    for j in range(ff // (2 * rows)):
        at = pl.ds(j * 2 * rows, 2 * rows)

        @pl.loop(0, d, step=block)
        def _(i):
            cols = pl.ds(pl.multiple_of(i, block), block)
            slots[j, :, cols] = wacc[at, cols].astype(BF16)
        out_copies.append(pltpu.make_async_copy(slots.at[j], dw.at[at], out_sem.at[j]))
        out_copies[-1].start()
    for c in out_copies + grads_copies(chips - 2) + grads_copies(chips - 1):
        c.wait()


def gather_hidden(k, dy, gate, up, w_down):
    (rows, d), (tokens, ff) = dy.shape, gate.shape
    dma = pltpu.SemaphoreType.DMA
    copies = (2, 2, 2 * RINGS)
    return pl.pallas_call(
        functools.partial(hidden_kernel, k),
        out_shape=[jax.ShapeDtypeStruct((tokens, ff), BF16)] * 2 + [jax.ShapeDtypeStruct((ff, d), BF16)],
        in_specs=[pl.BlockSpec(memory_space=pl.ANY)] * 4,
        out_specs=[pl.BlockSpec(memory_space=pl.ANY)] * 3,
        scratch_shapes=[
            pltpu.VMEM((4, ff, d // 4), BF16),
            pltpu.VMEM((ff, d), F32),
            pltpu.VMEM((2 * rows, ff), F32),
            pltpu.VMEM((2, 2, 2 * rows, ff), BF16),
            pltpu.VMEM((2 * rows, ff), BF16),
            pltpu.VMEM((2, 2, 2 * rows, ff), BF16),
            dma((4,)), dma(copies), dma(copies), dma((ff // (2 * rows),)),
            *gather_scratch(rows, d),
        ],
        compiler_params=pltpu.CompilerParams(collective_id=1, has_side_effects=True, vmem_limit_bytes=63 * 2**20),
        cost_estimate=pl.CostEstimate(flops=4 * tokens * ff * d, bytes_accessed=8 * tokens * ff, transcendentals=0),
        name="gather_hidden",
    )(dy, gate, up, w_down)


PASSES = 2
PIECES = 8


def weights_kernel(k, x, dg, du, dw_gate, dw_up, acc, grads, stage, *rest):
    (grads_sem, out_sem), comm = rest[:2], rest[2:]
    slots = comm[0]
    chips, rows, ff = k * k, x.shape[0], dg.shape[1]
    share, cols = rows // RINGS, slots.shape[2]
    core, a, b, positions = place(k)
    total = PASSES * chips
    high = cols // PIECES

    def grads_copies(g):
        return [
            pltpu.make_async_copy(t.at[pl.ds(at, share)], grads.at[g % 2, pl.ds(to, share), pl.ds(j * ff, ff)], grads_sem.at[g % 2, j, i])
            for i, (to, at) in enumerate(token_rows(k, positions, g, share, rows)) for j, t in enumerate((dg, du))]

    def out_copies(g, i):
        at = pl.ds(pl.multiple_of(g // chips * cols + i * high, high), high)
        return [pltpu.make_async_copy(stage.at[i, :, pl.ds(j * ff, ff)], t.at[at], out_sem.at[j, i]) for j, t in enumerate((dw_gate, dw_up))]

    for c in grads_copies(0):
        c.start()

    def before(g):
        @pl.when(g + 1 < total)
        def _():
            for c in grads_copies(g + 1):
                c.start()
        for c in grads_copies(g):
            c.wait()

    def piece(g, i):
        at = pl.ds(i * high, high)
        term = lax.dot_general(slots[g % SLOTS, :, at], grads[g % 2], (((0,), (0,)), ((), ())), preferred_element_type=F32)
        first, last = g % chips == 0, g % chips == chips - 1

        @pl.when(first)
        def _():
            acc[at] = term

        @pl.when(jnp.logical_not(first))
        def _():
            acc[at] += term

        @pl.when(last)
        def _():
            @pl.when(g >= chips)
            def _():
                for c in out_copies(g - chips, i):
                    c.wait()
            stage[i] = acc[at].astype(BF16)
            for c in out_copies(g, i):
                c.start()

    def some(h):
        def run(g):
            for i in range(h * PIECES // HALVES, (h + 1) * PIECES // HALVES):
                piece(g, i)
        return run

    gather(k, PASSES, core, a, b, positions, x, *comm, before, [some(h) for h in range(HALVES)], lambda g: None)
    for i in range(PIECES):
        for c in out_copies(total - 1, i):
            c.wait()


def gather_weights(k, x, dg, du):
    (rows, d), (tokens, ff) = x.shape, dg.shape
    cols = d // PASSES
    dma = pltpu.SemaphoreType.DMA
    return pl.pallas_call(
        functools.partial(weights_kernel, k),
        out_shape=[jax.ShapeDtypeStruct((d, ff), BF16)] * 2,
        in_specs=[pl.BlockSpec(memory_space=pl.ANY)] * 3,
        out_specs=[pl.BlockSpec(memory_space=pl.ANY)] * 2,
        scratch_shapes=[
            pltpu.VMEM((cols, 2 * ff), F32),
            pltpu.VMEM((2, 2 * rows, 2 * ff), BF16),
            pltpu.VMEM((PIECES, cols // PIECES, 2 * ff), BF16),
            dma((2, 2, 2 * RINGS)), dma((2, PIECES)),
            *gather_scratch(rows, cols),
        ],
        compiler_params=pltpu.CompilerParams(collective_id=2, has_side_effects=True, vmem_limit_bytes=63 * 2**20),
        cost_estimate=pl.CostEstimate(flops=4 * tokens * ff * d, bytes_accessed=8 * tokens * ff, transcendentals=0),
        name="gather_weights",
    )(x, dg, du)


def solution(mesh):
    k = math.isqrt(mesh.shape["tp"] // 2)

    def body(x, dy, gate, up, w_gate, w_up, w_down):
        d_gate, d_up, dw_down = gather_hidden(k, dy, gate, up, w_down)
        dw_gate, dw_up = gather_weights(k, x, d_gate, d_up)
        dx = scatter_dx(k, d_gate, d_up, w_gate, w_up)
        return dx, dw_gate, dw_up, dw_down

    rows, cols, grads = P(("dp", "tp"), None), P("dp", "tp"), P("dp", "tp")
    return jax.shard_map(
        body, mesh=mesh,
        in_specs=(rows, rows, cols, cols, P(None, "tp"), P(None, "tp"), P("tp", None)),
        out_specs=(rows, grads, grads, P(("dp", "tp"), None)), check_vma=False)
```

time: 741 us -> 691 us (0.933); the launches traced: 731 us -> 690 us
  Pallas kernels: 0 us -> 660 us
  matrix products: 431 us -> 0 us
  waiting for transfers between devices: 253 us -> 0 us
  between operations: 14 us -> 0.66 us
    pallas_call x0 -> x3, Pallas kernels: none -> 660 us  [the longest x1 270 us: gather_weights(): pl.pallas_call(functools.partial(weights_kernel, k), out_shape=[jax.Shape...]
    dot_general x6 -> x0, matrix products: 431 us -> none  [the longest x3 200 us: by_group(): jnp.einsum('gta,gtb->gab', a, b, preferred_element_type=jnp.float32)]
    unnamed x6 -> x0, waiting for transfers between devices: 253 us -> none
    unnamed x2 -> x12, local copies, waits for them, and re-layouts: 33.2 us -> 29.1 us
  transfers between devices with their start and end apart: 3 -> 0, of which waited for: 2 -> 0; matrix products, arithmetic and copies ran while one was open for 63% -> 0% of each run, Pallas kernels for 0% -> 0%
where the time goes in v1:
time: 691 us; the launch traced here: 690 us
  Pallas kernels  660 us (96%)
  local copies, waits for them, and re-layouts  29.1 us (4%)
    pallas_call x1, Pallas kernels, gather_weights(): pl.pallas_call(functools.partial(weights_kernel, k), out_shape=[jax.Shape...  270 us
    pallas_call x1, Pallas kernels, gather_hidden(): pl.pallas_call(functools.partial(hidden_kernel, k), out_shape=[jax.ShapeD...  203 us
    pallas_call x1, Pallas kernels, scatter_dx(): pl.pallas_call(functools.partial(scatter_kernel, k), out_shape=jax.ShapeD...  188 us
    unnamed x12, local copies, waits for them, and re-layouts  29.1 us

profile of v1, /device:TPU:97, one launch (start us, length us, event | category | flops | bytes accessed | tf_op | source)
XLA Modules:
  0.0 690.1 jit_solution(15298302039551329129)
XLA Ops:
  0.6 202.6 %gather_hidden.1 = (bf16[4096,768]{1,0:T(8,128)(2,1)}, bf16[4096,768]{1,0:T(8,128)(2,1)}, bf16[768,8192]{1,0:T(8,128)(2,1)}) custom-call(bf16[128,8192]{1,0:T(8,128)(2,1)} %dy.1, bf16[4096,768]{1,0:T(8,128)(2,1)} %gate.1, bf16[4096,768]{1,0:T(8,128)(2,1)} %up.1, bf16[768,8192]{1,0:T(8,128)(2,1)} %w_down.1), custom_call_target="tpu_custom_call" | custom-call | flops 103079215104 | bytes 25165824 | tf_op jit(solution)/shard_map/gather_hidden/pallas_call | solution.py:377
  203.3 187.9 %scatter_dx.1 = bf16[128,8192]{1,0:T(8,128)(2,1)} custom-call(bf16[4096,768]{1,0:T(8,128)(2,1)} %get-tuple-element.9.dg, bf16[4096,768]{1,0:T(8,128)(2,1)} %get-tuple-element.10.du, bf16[8192,768]{1,0:T(8,128)(2,1)} %wg.1, bf16[8192,768]{1,0:T(8,128)(2,1)} %wu.1), custom_call_target="tpu_custom_call" | custom-call | flops 103079215104 | bytes 44040192 | tf_op jit(solution)/shard_map/scatter_dx/pallas_call | solution.py:160
  391.2 269.8 %gather_weights.1 = (bf16[8192,768]{1,0:T(8,128)(2,1)}, bf16[8192,768]{1,0:T(8,128)(2,1)}) custom-call(bf16[128,8192]{1,0:T(8,128)(2,1)} %x.1, bf16[4096,768]{1,0:T(8,128)(2,1)} %get-tuple-element.9.dg, bf16[4096,768]{1,0:T(8,128)(2,1)} %get-tuple-element.10.du), custom_call_target="tpu_custom_call" | custom-call | flops 103079215104 | bytes 25165824 | tf_op jit(solution)/shard_map/gather_weights/pallas_call | solution.py:470
  661.0 3.1 copy.15
  664.1 0.0 copy-start
  664.1 0.0 slice-start
  664.1 0.0 slice-start.1
  664.1 12.3 %copy.16 = bf16[8192,768]{1,0:T(8,128)(2,1)} copy(bf16[8192,768]{1,0:T(8,128)(2,1)} %get-tuple-element.19) | data formatting | bytes 25165824
  676.4 0.0 copy-done
  676.4 0.0 slice-start.2
  676.4 6.4 copy.17
  682.8 0.0 slice-done
  682.8 1.2 slice-done.1
  684.0 1.3 slice-done.2
  685.3 4.8 copy.18
  (1 shorter events, 0.0 us)
Async XLA Ops:
  664.1 12.3 %copy-start = (bf16[8192,768]{1,0:T(8,128)(2,1)S(1)}, bf16[8192,768]{1,0:T(8,128)(2,1)}, u32[]{:S(2)}) copy-start(bf16[8192,768]{1,0:T(8,128)(2,1)} %get-tuple-element.20) | copy-start | bytes 37748740
  664.1 18.7 %slice-start = ((s8[12582912]{0:T(1024)(128)(4,1)}), s8[4194304]{0:T(1024)(128)(4,1)S(1)}, s32[]{:S(2)}) async-start(s8[12582912]{0:T(1024)(128)(4,1)} %bitcast), calls=%async_computation | async-start | bytes 8388608
  664.1 19.9 %slice-start.1 = ((s8[12582912]{0:T(1024)(128)(4,1)}), s8[4194304]{0:T(1024)(128)(4,1)S(1)}, s32[]{:S(2)}) async-start(s8[12582912]{0:T(1024)(128)(4,1)} %bitcast), calls=%async_computation.1 | async-start | bytes 8388608
  676.4 8.9 %slice-start.2 = ((s8[12582912]{0:T(1024)(128)(4,1)}), s8[4194304]{0:T(1024)(128)(4,1)S(1)}, s32[]{:S(2)}) async-start(s8[12582912]{0:T(1024)(128)(4,1)} %bitcast), calls=%async_computation.2 | async-start | bytes 8388608

commit v2 on v1

v2 whole, which is shorter than its diff:
```python
import functools
import math

import jax
import jax.numpy as jnp
from jax import lax
from jax.experimental import pallas as pl
from jax.experimental.pallas import tpu as pltpu
from jax.sharding import PartitionSpec as P

F32, BF16 = jnp.float32, jnp.bfloat16
RINGS = 4
PARTS = 2
FETCH = 3
LEAD = 4


def act(gate, up):
    return jax.nn.silu(gate) * up


def place(k):
    me = lax.axis_index("tp")
    core, chip = me % 2, me // 2
    a, b = chip // k, chip % k
    s = (a + b) % k
    return core, a, b, (a * k + s, b * k + s)


def chip_at(k, cycle, position):
    a = position // k
    b = (position % k - a + k) % k
    return a * k + b if cycle == 0 else b * k + a


def on_ring(ring, position, steps, chips):
    return (position + steps + chips) % chips if ring % 2 == 0 else (position - steps + chips) % chips


def greet(k, core, a, b):
    chips = (((a + 1) % k) * k + b, ((a + k - 1) % k) * k + b, a * k + (b + 1) % k, a * k + (b + k - 1) % k)
    barrier = pltpu.get_barrier_semaphore()
    for chip in chips:
        pl.semaphore_signal(barrier, inc=1, device_id={"tp": chip * 2 + core})
    pl.semaphore_signal(barrier, inc=1, device_id={"tp": (a * k + b) * 2 + 1 - core})
    pl.semaphore_wait(barrier, 5)


def scatter_kernel(k, grads, wg, wu, out, wv, av, own, psend, precv, rsend, rrecv,
                   w_sem, a_sem, psend_sem, precv_sem, rsend_sem, rrecv_sem, out_sem):
    chips = k * k
    units, width, depth = wv.shape
    rows, ff = out.shape[0], depth // 2
    core, a, b, positions = place(k)
    partner = (a * k + b) * 2 + 1 - core
    order = [(r * PARTS + h, r, h) for h in range(PARTS) for r in range(RINGS)]

    def w_copies(u):
        cols = pl.ds(u * width, width)
        return [pltpu.make_async_copy(w.at[cols], wv.at[u, :, pl.ds(i * ff, ff)], w_sem.at[u, i]) for i, w in enumerate((wg, wu))]

    def a_copies(s, r):
        to = chip_at(k, r // 2, on_ring(r, positions[r // 2], -1 - s + chips, chips))
        copies = []
        for i, which in enumerate((core, 1 - core)):
            at = pl.ds((to * 2 + which) * rows, rows)
            copies.append(pltpu.make_async_copy(grads.at[at], av.at[s % 2, r, pl.ds(i * rows, rows)], a_sem.at[s % 2, r, i]))
        return copies

    def to_partner(s, u):
        return pltpu.make_async_remote_copy(
            psend.at[u], precv.at[s % 2, u], psend_sem.at[u], precv_sem.at[s % 2, u], device_id={"tp": partner})

    def to_next(s, u, r):
        to = chip_at(k, r // 2, on_ring(r, positions[r // 2], 1, chips)) * 2 + core
        return pltpu.make_async_remote_copy(
            rsend.at[s % 2, u], rrecv.at[(s + 1) % 3, u], rsend_sem.at[s % 2, u], rrecv_sem.at[(s + 1) % 3, u], device_id={"tp": to})

    def to_out(u):
        return pltpu.make_async_copy(rsend.at[(chips - 1) % 2, u], out.at[:, pl.ds(u * width, width)], out_sem.at[u])

    def multiply(s, u, r, h, first=False):
        if first:
            for c in w_copies(u):
                c.wait()
        if h == 0:
            for c in a_copies(s, r):
                c.wait()
        if not first:
            to_partner(s, u).wait_send()
        acc = lax.dot_general(av[s % 2, r], wv[u], (((1,), (1,)), ((), ())), preferred_element_type=F32)
        own[u] = acc[:rows]
        psend[u] = acc[rows:].astype(BF16)
        to_partner(s, u).start()

    def combine(s, u, r):
        to_partner(s, u).wait_recv()

        @pl.when(s >= 2)
        def _():
            to_next(s, u, r).wait_send()

        @pl.when(s == 0)
        def _():
            rsend[s % 2, u] = (own[u] + precv[s % 2, u].astype(F32)).astype(BF16)

        @pl.when(s > 0)
        def _():
            to_next(s - 1, u, r).wait_recv()
            rsend[s % 2, u] = (own[u] + precv[s % 2, u].astype(F32) + rrecv[s % 3, u].astype(F32)).astype(BF16)

        @pl.when(s < chips - 1)
        def _():
            to_next(s, u, r).start()

        @pl.when(s == chips - 1)
        def _():
            to_out(u).start()

    def fetch(i):
        if i < units:
            u, r, h = order[i]
            for c in (a_copies(0, r) if h == 0 else []) + w_copies(u):
                c.start()

    for i in range(FETCH):
        fetch(i)
    greet(k, core, a, b)
    for i, (u, r, h) in enumerate(order):
        fetch(i + FETCH)
        multiply(0, u, r, h, first=True)
        if i >= LEAD:
            combine(0, *order[i - LEAD][:2])
        if h == PARTS - 1:
            for c in a_copies(1, r):
                c.start()

    @pl.loop(0, chips)
    def _(s):
        @pl.when(s + 2 < chips)
        def _():
            for r in range(RINGS):
                for c in a_copies(s + 2, r):
                    c.start()
        for i, (u, r, h) in enumerate(order):
            late = units - LEAD + i

            @pl.when(s + 1 < chips)
            def _():
                multiply(s + 1, u, r, h)
            if late < units:
                combine(s, *order[late][:2])
            else:
                @pl.when(s + 1 < chips)
                def _():
                    combine(s + 1, *order[late - units][:2])

    for u, r, h in order:
        to_partner(chips - 1, u).wait_send()
        to_next(chips - 2, u, r).wait_send()
        to_out(u).wait()


def scatter_dx(k, grads, wg, wu):
    tokens, (d, ff) = grads.shape[0], wg.shape
    rows = tokens // (2 * k * k)
    units = RINGS * PARTS
    width = d // units
    dma = pltpu.SemaphoreType.DMA
    return pl.pallas_call(
        functools.partial(scatter_kernel, k),
        out_shape=jax.ShapeDtypeStruct((rows, d), BF16),
        in_specs=[pl.BlockSpec(memory_space=pl.ANY)] * 3,
        out_specs=pl.BlockSpec(memory_space=pl.ANY),
        scratch_shapes=[
            pltpu.VMEM((units, width, 2 * ff), BF16),
            pltpu.VMEM((2, RINGS, 2 * rows, 2 * ff), BF16),
            pltpu.VMEM((units, rows, width), F32),
            pltpu.VMEM((units, rows, width), BF16),
            pltpu.VMEM((2, units, rows, width), BF16),
            pltpu.VMEM((2, units, rows, width), BF16),
            pltpu.VMEM((3, units, rows, width), BF16),
            dma((units, 2)), dma((2, RINGS, 2)), dma((units,)), dma((2, units)), dma((2, units)), dma((3, units)), dma((units,)),
        ],
        compiler_params=pltpu.CompilerParams(collective_id=0, has_side_effects=True, vmem_limit_bytes=63 * 2**20),
        cost_estimate=pl.CostEstimate(flops=4 * tokens * ff * d, bytes_accessed=6 * tokens * ff + 4 * d * ff, transcendentals=0),
        name="scatter_dx",
    )(grads, wg, wu)


SLOTS = 4


def gather(k, passes, core, a, b, positions, src, slots, load_sem, next_sem, ring_sem, mate_send_sem, mate_sem, credit, before, pieces):
    chips = k * k
    total = passes * chips
    share, cols = slots.shape[1] // (2 * RINGS), slots.shape[2]
    width = cols // PARTS
    partner = (a * k + b) * 2 + 1 - core

    def part(g, r, h, which=core):
        at = pl.multiple_of((2 * r + which) * share, share)
        return slots.at[g % SLOTS, pl.ds(at, share), pl.ds(h * width, width)]

    def load(g, r, h):
        at = pl.multiple_of(g // chips * cols + h * width, width)
        return pltpu.make_async_copy(src.at[pl.ds(r * share, share), pl.ds(at, width)], part(g, r, h), load_sem.at[r, h])

    def to_next(g, r, h):
        to = chip_at(k, r // 2, on_ring(r, positions[r // 2], 1, chips)) * 2 + core
        return pltpu.make_async_remote_copy(
            part(g, r, h), part(g + 1, r, h), next_sem.at[g % SLOTS, r, h], ring_sem.at[(g + 1) % SLOTS, r, h], device_id={"tp": to})

    def to_mate(g, r, h):
        return pltpu.make_async_remote_copy(
            part(g, r, h), part(g, r, h), mate_send_sem.at[g % 2, r, h], mate_sem.at[g % SLOTS, r, h], device_id={"tp": partner})

    def came_from_mate(g, r, h):
        return pltpu.make_async_remote_copy(
            part(g, r, h), part(g, r, h, 1 - core), mate_send_sem.at[g % 2, r, h], mate_sem.at[g % SLOTS, r, h], device_id={"tp": partner})

    def pass_on(g, r, h):
        @pl.when(g == 0)
        def _():
            load(g, r, h).wait()

        @pl.when(g % chips > 0)
        def _():
            to_next(g - 1, r, h).wait_recv()

        early = jnp.where(g % chips == chips - 1, 1, 0)
        goes = jnp.where(g % chips == 0, jnp.where(g == 0, 1, 0), jnp.where(g + early < total, 1, 0))

        @pl.when(goes == 1)
        def _():
            @pl.when(early == 1)
            def _():
                load(g + 1, r, h).wait()
            if h == 0:
                @pl.when(g + early + 1 >= SLOTS)
                def _():
                    pl.semaphore_wait(credit.at[r], 1)
            to_next(g + early, r, h).start()

    both = [(r, h) for h in range(PARTS) for r in range(RINGS)]
    for r, h in both:
        load(0, r, h).start()
    greet(k, core, a, b)

    def pass_all(g, h):
        for r in range(RINGS):
            pass_on(g, r, h)
        for r in range(RINGS):
            to_mate(g, r, h).start()

    def compute(g, h):
        for r in range(RINGS):
            came_from_mate(g, r, h).wait_recv()
        pieces[h](g)

    @pl.loop(0, total + 1)
    def _(g):
        @pl.when(g == 0)
        def _():
            for h in range(PARTS):
                pass_all(g, h)
            before()

        for h in range(PARTS):
            @pl.when(jnp.logical_and(g > 0, g < total))
            def _():
                pass_all(g, h)

            @pl.when(g > 0 if h == 0 else g < total)
            def _():
                compute(g - 1 if h == 0 else g, (h - 1) % PARTS)

        @pl.when(g > 0)
        def _():
            for r, h in both:
                @pl.when((g - 1) % chips < chips - 1)
                def _():
                    to_next(g - 1, r, h).wait_send()
                to_mate(g - 1, r, h).wait_send()
            refill = g - 1 + SLOTS

            @pl.when(jnp.logical_and(refill < total, refill % chips > 0))
            def _():
                for r in range(RINGS):
                    frm = chip_at(k, r // 2, on_ring(r, positions[r // 2], -1, chips)) * 2 + core
                    pl.semaphore_signal(credit.at[r], inc=1, device_id={"tp": frm})

            @pl.when(jnp.logical_and(refill < total, refill % chips == 0))
            def _():
                for r, h in both:
                    load(refill, r, h).start()


def gather_scratch(rows, cols):
    dma, two = pltpu.SemaphoreType.DMA, (2, RINGS, PARTS)
    return [
        pltpu.VMEM((SLOTS, 2 * rows, cols), BF16),
        dma((RINGS, PARTS)), dma((SLOTS, RINGS, PARTS)), dma((SLOTS, RINGS, PARTS)), dma(two), dma((SLOTS, RINGS, PARTS)),
        pltpu.SemaphoreType.REGULAR((RINGS,)),
    ]


def token_rows(k, positions, g, share, rows):
    chips = k * k
    for r in range(RINGS):
        chip = chip_at(k, r // 2, on_ring(r, positions[r // 2], -(g % chips), chips))
        for c in range(2):
            yield (2 * r + c) * share, pl.multiple_of((chip * 2 + c) * rows + r * share, share)


def hidden_kernel(k, dy, gate, up, w_down, all_grads, dw, wd, wacc, hacc, given, hid, hid_t, grads, *rest):
    (w_sem, given_sem, grads_sem, out_sem), comm = rest[:4], rest[4:]
    slots = comm[0]
    chips, (rows, d), ff = k * k, dy.shape, gate.shape[1]
    share = rows // RINGS
    core, a, b, positions = place(k)
    quarter = d // PARTS
    block = d // 16

    def given_copies(g):
        return [
            pltpu.make_async_copy(t.at[pl.ds(at, share)], given.at[g % 2, j, pl.ds(to, share)], given_sem.at[g % 2, j, i])
            for i, (to, at) in enumerate(token_rows(k, positions, g, share, rows)) for j, t in enumerate((gate, up))]

    def grads_copies(g):
        return [
            pltpu.make_async_copy(grads.at[g % 2, pl.ds(to, share)], all_grads.at[pl.ds(at, share)], grads_sem.at[g % 2, i])
            for i, (to, at) in enumerate(token_rows(k, positions, g, share, rows))]

    w_copies = [pltpu.make_async_copy(w_down.at[:, pl.ds(i * quarter, quarter)], wd.at[i], w_sem.at[i]) for i in range(PARTS)]

    def before():
        for c in given_copies(0) + w_copies:
            c.start()

        @pl.loop(0, ff, step=64)
        def _(i):
            wacc[pl.ds(pl.multiple_of(i, 64), 64)] = jnp.zeros((64, d), F32)
        for c in w_copies:
            c.wait()

    def d_hidden(g, i):
        term = lax.dot_general(slots[g % SLOTS, :, pl.ds(i * quarter, quarter)], wd[i], (((1,), (1,)), ((), ())), preferred_element_type=F32)
        hacc[...] = term if i == 0 else hacc[...] + term

    def piece(i):
        def run(g):
            if i == 0:
                @pl.when(g + 1 < chips)
                def _():
                    for c in given_copies(g + 1):
                        c.start()
            d_hidden(g, i)
            if i == PARTS - 1:
                last(g)
        return run

    def last(g):
        for c in given_copies(g):
            c.wait()

        @pl.when(g >= 2)
        def _():
            for c in grads_copies(g - 2):
                c.wait()

        @pl.loop(0, 2 * rows, step=2 * share)
        def _(i):
            at = pl.ds(pl.multiple_of(i, 2 * share), 2 * share)
            hidden, back = jax.vjp(act, given[g % 2, 0, at].astype(F32), given[g % 2, 1, at].astype(F32))
            for j, t in enumerate(back(hacc[at])):
                grads[g % 2, at, pl.ds(j * ff, ff)] = t.astype(BF16)
            hid[at] = hidden.astype(BF16)
        for c in grads_copies(g):
            c.start()
        hid_t[...] = hid[...].T

        def term(at):
            return wacc[:, at] + jnp.dot(hid_t[...], slots[g % SLOTS, :, at], preferred_element_type=F32)

        @pl.when(g < chips - 1)
        def _():
            @pl.loop(0, d, step=block)
            def _(i):
                at = pl.ds(pl.multiple_of(i, block), block)
                wacc[:, at] = term(at)

        @pl.when(g == chips - 1)
        def _():
            @pl.loop(0, d // block)
            def _(i):
                at = pl.ds(pl.multiple_of(i * block, block), block)
                done = term(at).astype(BF16)
                for j in range(ff // (2 * rows)):
                    slots[j, :, at] = done[2 * rows * j:2 * rows * (j + 1)]
                    out_copy(i, j).start()

    def out_copy(i, j):
        at = pl.ds(pl.multiple_of(i * block, block), block)
        return pltpu.make_async_copy(slots.at[j, :, at], dw.at[pl.ds(2 * rows * j, 2 * rows), at], out_sem.at[i, j])

    gather(k, 1, core, a, b, positions, dy, *comm, before, [piece(i) for i in range(PARTS)])

    @pl.loop(0, d // block)
    def _(i):
        for j in range(ff // (2 * rows)):
            out_copy(i, j).wait()
    for c in grads_copies(chips - 2) + grads_copies(chips - 1):
        c.wait()


def gather_hidden(k, dy, gate, up, w_down):
    (rows, d), (tokens, ff) = dy.shape, gate.shape
    dma = pltpu.SemaphoreType.DMA
    copies = (2, 2, 2 * RINGS)
    return pl.pallas_call(
        functools.partial(hidden_kernel, k),
        out_shape=[jax.ShapeDtypeStruct((tokens, 2 * ff), BF16), jax.ShapeDtypeStruct((ff, d), BF16)],
        in_specs=[pl.BlockSpec(memory_space=pl.ANY)] * 4,
        out_specs=[pl.BlockSpec(memory_space=pl.ANY)] * 2,
        scratch_shapes=[
            pltpu.VMEM((PARTS, ff, d // PARTS), BF16),
            pltpu.VMEM((ff, d), F32),
            pltpu.VMEM((2 * rows, ff), F32),
            pltpu.VMEM((2, 2, 2 * rows, ff), BF16),
            pltpu.VMEM((2 * rows, ff), BF16),
            pltpu.VMEM((ff, 2 * rows), BF16),
            pltpu.VMEM((2, 2 * rows, 2 * ff), BF16),
            dma((PARTS,)), dma(copies), dma((2, 2 * RINGS)), dma((16, ff // (2 * rows))),
            *gather_scratch(rows, d),
        ],
        compiler_params=pltpu.CompilerParams(collective_id=1, has_side_effects=True, vmem_limit_bytes=63 * 2**20),
        cost_estimate=pl.CostEstimate(flops=4 * tokens * ff * d, bytes_accessed=8 * tokens * ff, transcendentals=0),
        name="gather_hidden",
    )(dy, gate, up, w_down)


PASSES = 2
PIECES = 8


def weights_kernel(k, x, all_grads, dw_gate, dw_up, acc, grads, stage, *rest):
    (grads_sem, out_sem), comm = rest[:2], rest[2:]
    slots = comm[0]
    chips, rows, ff = k * k, x.shape[0], dw_gate.shape[1]
    share, cols = rows // RINGS, slots.shape[2]
    core, a, b, positions = place(k)
    total = PASSES * chips
    high = cols // PIECES

    def grads_copies(g):
        return [
            pltpu.make_async_copy(all_grads.at[pl.ds(at, share)], grads.at[g % 2, pl.ds(to, share)], grads_sem.at[g % 2, i])
            for i, (to, at) in enumerate(token_rows(k, positions, g, share, rows))]

    def out_copies(g, i):
        at = pl.ds(pl.multiple_of(g // chips * cols + i * high, high), high)
        return [pltpu.make_async_copy(stage.at[i, :, pl.ds(j * ff, ff)], t.at[at], out_sem.at[j, i]) for j, t in enumerate((dw_gate, dw_up))]

    def before():
        for c in grads_copies(0):
            c.start()

        @pl.loop(0, cols, step=high)
        def _(i):
            acc[pl.ds(pl.multiple_of(i, high), high)] = jnp.zeros((high, 2 * ff), F32)

    def piece(g, i):
        at = pl.ds(i * high, high)
        acc[at] += lax.dot_general(slots[g % SLOTS, :, at], grads[g % 2], (((0,), (0,)), ((), ())), preferred_element_type=F32)

        @pl.when(g % chips == chips - 1)
        def _():
            @pl.when(g >= chips)
            def _():
                for c in out_copies(g - chips, i):
                    c.wait()
            stage[i] = acc[at].astype(BF16)
            acc[at] = jnp.zeros((high, 2 * ff), F32)
            for c in out_copies(g, i):
                c.start()

    def some(h):
        def run(g):
            if h == 0:
                @pl.when(g + 1 < total)
                def _():
                    for c in grads_copies(g + 1):
                        c.start()
                for c in grads_copies(g):
                    c.wait()
            for i in range(h * PIECES // PARTS, (h + 1) * PIECES // PARTS):
                piece(g, i)
        return run

    gather(k, PASSES, core, a, b, positions, x, *comm, before, [some(h) for h in range(PARTS)])
    for i in range(PIECES):
        for c in out_copies(total - 1, i):
            c.wait()


def gather_weights(k, x, grads):
    (rows, d), (tokens, ff) = x.shape, (grads.shape[0], grads.shape[1] // 2)
    cols = d // PASSES
    dma = pltpu.SemaphoreType.DMA
    return pl.pallas_call(
        functools.partial(weights_kernel, k),
        out_shape=[jax.ShapeDtypeStruct((d, ff), BF16)] * 2,
        in_specs=[pl.BlockSpec(memory_space=pl.ANY)] * 2,
        out_specs=[pl.BlockSpec(memory_space=pl.ANY)] * 2,
        scratch_shapes=[
            pltpu.VMEM((cols, 2 * ff), F32),
            pltpu.VMEM((2, 2 * rows, 2 * ff), BF16),
            pltpu.VMEM((PIECES, cols // PIECES, 2 * ff), BF16),
            dma((2, 2 * RINGS)), dma((2, PIECES)),
            *gather_scratch(rows, cols),
        ],
        compiler_params=pltpu.CompilerParams(collective_id=2, has_side_effects=True, vmem_limit_bytes=63 * 2**20),
        cost_estimate=pl.CostEstimate(flops=4 * tokens * ff * d, bytes_accessed=8 * tokens * ff, transcendentals=0),
        name="gather_weights",
    )(x, grads)


def hand_over_kernel(*refs):
    count = len(refs) // 3
    arrays, (load_sem, store_sem) = list(zip(refs[:count], refs[count:2 * count], refs[2 * count:3 * count])), refs[3 * count:]
    moves = []
    for i, (src, dst, mid) in enumerate(arrays):
        high = src.shape[0] // PIECES
        for j in range(PIECES):
            at = pl.ds(j * high, high)
            moves.append((pltpu.make_async_copy(src.at[at], mid.at[at], load_sem.at[i, j]),
                          pltpu.make_async_copy(mid.at[at], dst.at[at], store_sem.at[i, j])))
    for load, _ in moves:
        load.start()
    for load, store in moves:
        load.wait()
        store.start()
    for _, store in moves:
        store.wait()


def hand_over(*arrays):
    dma = pltpu.SemaphoreType.DMA((len(arrays), PIECES))
    return pl.pallas_call(
        hand_over_kernel,
        out_shape=[jax.ShapeDtypeStruct(t.shape, t.dtype) for t in arrays],
        in_specs=[pl.BlockSpec(memory_space=pl.ANY)] * len(arrays),
        out_specs=[pl.BlockSpec(memory_space=pl.ANY)] * len(arrays),
        scratch_shapes=[*(pltpu.VMEM(t.shape, t.dtype) for t in arrays), dma, dma],
        compiler_params=pltpu.CompilerParams(vmem_limit_bytes=63 * 2**20),
        name="hand_over",
    )(*arrays)


def solution(mesh):
    k = math.isqrt(mesh.shape["tp"] // 2)

    def body(x, dy, gate, up, w_gate, w_up, w_down):
        grads, dw_down = gather_hidden(k, dy, gate, up, w_down)
        dw_gate, dw_up = gather_weights(k, x, grads)
        dx = scatter_dx(k, grads, w_gate, w_up)
        return tuple(hand_over(dx, dw_gate, dw_up, dw_down))

    rows, cols, sums = P(("dp", "tp"), None), P("dp", "tp"), P("dp", "tp")
    return jax.shard_map(
        body, mesh=mesh,
        in_specs=(rows, rows, cols, cols, P(None, "tp"), P(None, "tp"), P("tp", None)),
        out_specs=(rows, sums, sums, P(("dp", "tp"), None)), check_vma=False)
```

time: 691 us -> 602 us (0.87)
  Pallas kernels: 660 us -> 601 us
  local copies, waits for them, and re-layouts: 29.1 us -> 0 us
    pallas_call x1, Pallas kernels: 270 us -> 196 us  [gather_weights(): pl.pallas_call(functools.partial(weights_kernel, k), out_shape=[jax.Shape...]
    unnamed x12 -> x0, local copies, waits for them, and re-layouts: 29.1 us -> none
    pallas_call x0 -> x1, Pallas kernels: none -> 26.5 us  [hand_over(): pl.pallas_call(hand_over_kernel, out_shape=[jax.ShapeDtypeStruct(t.shape,...]
    pallas_call x1, Pallas kernels: 203 us -> 196 us  [gather_hidden(): pl.pallas_call(functools.partial(hidden_kernel, k), out_shape=[jax.ShapeD...]
where the time goes in v2:
time: 602 us
  Pallas kernels  601 us (100%)
    pallas_call x1, Pallas kernels, gather_weights(): pl.pallas_call(functools.partial(weights_kernel, k), out_shape=[jax.Shape...  196 us
    pallas_call x1, Pallas kernels, gather_hidden(): pl.pallas_call(functools.partial(hidden_kernel, k), out_shape=[jax.ShapeD...  196 us
    pallas_call x1, Pallas kernels, scatter_dx(): pl.pallas_call(functools.partial(scatter_kernel, k), out_shape=jax.ShapeD...  183 us
    pallas_call x1, Pallas kernels, hand_over(): pl.pallas_call(hand_over_kernel, out_shape=[jax.ShapeDtypeStruct(t.shape,...  26.5 us

profile of v2, /device:TPU:97, one launch (start us, length us, event | category | flops | bytes accessed | tf_op | source)
XLA Modules:
  0.0 602.0 jit_solution(15338500636356310946)
XLA Ops:
  0.6 195.5 %gather_hidden.1 = (bf16[4096,1536]{1,0:T(8,128)(2,1)}, bf16[768,8192]{1,0:T(8,128)(2,1)}) custom-call(bf16[128,8192]{1,0:T(8,128)(2,1)} %dy.1, bf16[4096,768]{1,0:T(8,128)(2,1)} %gate.1, bf16[4096,768]{1,0:T(8,128)(2,1)} %up.1, bf16[768,8192]{1,0:T(8,128)(2,1)} %w_down.1), custom_call_target="tpu_custom_call" | custom-call | flops 103079215104 | bytes 25165824 | tf_op jit(solution)/shard_map/gather_hidden/pallas_call | solution.py:421
  196.2 182.6 %scatter_dx.1.refs_0_ = bf16[128,8192]{1,0:T(8,128)(2,1)} custom-call(bf16[4096,1536]{1,0:T(8,128)(2,1)} %get-tuple-element.8.grads.all_grads, bf16[8192,768]{1,0:T(8,128)(2,1)} %wg.1, bf16[8192,768]{1,0:T(8,128)(2,1)} %wu.1), custom_call_target="tpu_custom_call" | custom-call | flops 103079215104 | bytes 44040192 | tf_op jit(solution)/shard_map/scatter_dx/pallas_call | solution.py:170
  378.8 196.5 %gather_weights.1 = (bf16[8192,768]{1,0:T(8,128)(2,1)}, bf16[8192,768]{1,0:T(8,128)(2,1)}) custom-call(bf16[128,8192]{1,0:T(8,128)(2,1)} %x.1, bf16[4096,1536]{1,0:T(8,128)(2,1)} %get-tuple-element.8.grads.all_grads), custom_call_target="tpu_custom_call" | custom-call | flops 103079215104 | bytes 25165824 | tf_op jit(solution)/shard_map/gather_weights/pallas_call | solution.py:511
  575.3 26.5 %hand_over.1 = (bf16[128,8192]{1,0:T(8,128)(2,1)}, bf16[8192,768]{1,0:T(8,128)(2,1)}, bf16[8192,768]{1,0:T(8,128)(2,1)}, bf16[768,8192]{1,0:T(8,128)(2,1)}) custom-call(bf16[128,8192]{1,0:T(8,128)(2,1)} %scatter_dx.1.refs_0_, bf16[8192,768]{1,0:T(8,128)(2,1)} %get-tuple-element.9.refs_1_, bf16[8192,768]{1,0:T(8,128)(2,1)} %get-tuple-element.10.refs_2_, ...), custom_call_target="tpu_custom_call" | custom-call | tf_op jit(solution)/shard_map/hand_over/pallas_call | solution.py:550
